TPU v7x, 256 devices: a 8x8x2 block of a 8x8x16 slice. The times are simulated.
256 devices in a mesh: groups: 2 (over z), owners: 16 (over x, core), sub: 8 (over y).
Axes of the slice: x: 8, y: 8, z: 2, core: 2. Of those that a mesh axis runs over, the one named last changes fastest.
The devices are a block of a 8x8x16 slice.
Arguments:
- embeddings: bfloat16 [131072, 768], P(('groups', 'owners', 'sub')), parts along dimension 0, may hold values from -6 to 6, as said below
- class_table: bfloat16 [1000, 768], replicated, may hold values from -6 to 6
- nearest: int32 [131072], P(('groups', 'owners', 'sub')), parts along dimension 0, may hold values from 0 to 999
- keep_class: int32 [1000], replicated, may hold values 0 or 1
- destination: int32 [131072, 1], P(('groups', 'owners', 'sub')), parts along dimension 0, may hold values from 0 to 127; in each aligned block of 512 rows (0 to 511, 512 to 1023, ...) at most 6 rows name the same one
Outputs:
- received_rows: bfloat16 [196608, 768], P(('groups', 'owners', 'sub')), parts along dimension 0
- received_score: bfloat16 [196608], P(('groups', 'owners', 'sub')), parts along dimension 0
- received_position: int32 [196608], P(('groups', 'owners', 'sub')), parts along dimension 0
- shard_totals: int32 [256], P('groups'), parts along dimension 0
There are 2 independent parts, one for each index of `groups`. A program takes and returns all parts, laid end to end along the dimension named above; an argument that names none is the same for every part. Nothing has to cross between parts.
Inputs may be any that keep to these rules, and one draw needn't show every extreme that they name: `destination`: in the rows of one device no loader shard is named by more than 6 rows. Counts of rows per loader shard may be packed several to an int32 word wherever they travel; this is an exception to the 16-bit rule below. `embeddings`: some rows are entirely zero.
All inputs are finite; a program needn't handle non-finite values.
Results may differ from a plain program's by a relative error of at most 0.001.
Values may be sent and summed in bfloat16 or wider, within the bound.
No kernel may reach another device: no remote copies, remote signals or barrier semaphores. Data moves between devices by JAX's collectives and lax.ppermute only.
A program may use at most 64 MiB of HBM per device.

v0:
```python
import math

import jax
import jax.numpy as jnp
from jax import lax
from jax.sharding import Mesh
from jax.sharding import PartitionSpec as P

OWNERS_SUB = ("owners_0", "owners_1", "sub")
GROUPS_OWNERS_SUB = ("groups", "owners_0", "owners_1", "sub")


def sent_together(arrays, axis, split_dim, concat_dim, along):
    columns = [a.reshape(*a.shape[:along], -1) for a in arrays]
    both = jnp.concatenate(columns, axis=along)
    result, at, finished = (
        lax.all_to_all(both, axis, split_axis=split_dim, concat_axis=concat_dim, tiled=True),
        0,
        [],
    )
    for a, column in zip(arrays, columns):
        slab = result[..., at : at + column.shape[along]]
        finished.append(slab.reshape(*slab.shape[:along], *a.shape[along:]))
        at += column.shape[along]
    return tuple(finished)


def laid_out(tiles, dim):
    tiles = jnp.moveaxis(tiles, 0, dim)
    shape = tiles.shape
    return tiles.reshape(*shape[:dim], shape[dim] * shape[dim + 1], *shape[dim + 2 :])


def stacked_from(value, axes, sequence):
    tiles = value
    for k in sequence:
        tiles = lax.all_gather(tiles, axes[k])
    done = sequence[::-1]
    back = [done.index(k) for k in range(len(axes))]
    tiles = tiles.transpose(*back, *range(len(axes), tiles.ndim))
    return tiles.reshape(-1, *value.shape)


def gathered_by_axis(value, axes, sequence, dim):
    return laid_out(stacked_from(value, axes, sequence), dim)


def margins(row_block, near_block, class_table, inverse_class, keep_class):
    products = lax.dot_general(
        row_block, class_table, (((1,), (1,)), ((), ())), preferred_element_type=jnp.float32
    )
    row_float = row_block.astype(jnp.float32)
    inverse_row = lax.rsqrt(jnp.sum(row_float * row_float, axis=1) + 1e-06)
    cosine = products * inverse_row[:, None] * inverse_class[None, :]
    class_ids = jnp.arange(class_table.shape[0], dtype=jnp.int32)
    class_match = near_block[:, None] == class_ids[None, :]
    given_cos = jnp.sum(jnp.where(class_match, cosine, 0.0), axis=1)
    others = jnp.max(jnp.where(class_match, -1e30, cosine), axis=1)
    kept_flag = jnp.sum(jnp.where(class_match, keep_class[None, :], 0), axis=1)
    return (20.0 * (given_cos - others), kept_flag)


def place_column(column, capacity):
    before = jnp.cumsum(column) - column
    offsets = jnp.arange(capacity, dtype=jnp.int32)
    placed = jnp.where(offsets[None, :] < column[:, None], before[:, None] + offsets[None, :], -1)
    return placed.reshape(column.shape[0] * capacity)


def on_device(embeddings, class_table, nearest, keep_class, destination):
    shard_count = lax.axis_size(OWNERS_SUB)
    local_rows = embeddings.shape[0]
    feature_width = embeddings.shape[1]
    capacity = 3 * local_rows // (2 * shard_count)
    class_float = class_table.astype(jnp.float32)
    inverse_class = lax.rsqrt(jnp.sum(class_float * class_float, axis=1) + 1e-06)
    block_rows = math.gcd(local_rows, 512)

    def one_block(inputs):
        return margins(inputs[0], inputs[1], class_table, inverse_class, keep_class)

    margin_value, kept_flag = lax.map(
        one_block,
        (
            embeddings.reshape(local_rows // block_rows, block_rows, feature_width),
            nearest.reshape(local_rows // block_rows, block_rows),
        ),
    )
    margin_value = margin_value.reshape(local_rows)
    kept_flag = kept_flag.reshape(local_rows)
    target = destination[:, 0]
    shard_ids = jnp.arange(shard_count, dtype=jnp.int32)
    onehot = ((target[:, None] == shard_ids[None, :]) & (kept_flag[:, None] == 1)).astype(jnp.int32)
    running = jnp.cumsum(onehot, axis=0) - onehot
    local_rank = jnp.sum(running * onehot, axis=1)
    counts = jnp.sum(onehot, axis=0)
    slot_index = jnp.where(kept_flag == 1, target * capacity + local_rank, shard_count * capacity)
    send_rows = (
        jnp.zeros((shard_count * capacity, feature_width), jnp.bfloat16)
        .at[slot_index]
        .set(embeddings, mode="drop")
    )
    send_score = (
        jnp.zeros((shard_count * capacity,), jnp.bfloat16)
        .at[slot_index]
        .set(margin_value.astype(jnp.bfloat16), mode="drop")
    )
    got_rows, got_score = sent_together(
        (
            send_rows.reshape(shard_count, capacity, feature_width),
            send_score.reshape(shard_count, capacity),
        ),
        OWNERS_SUB,
        0,
        0,
        2,
    )
    received_rows = got_rows.reshape(shard_count * capacity, feature_width)
    received_score = got_score.reshape(shard_count * capacity)
    all_counts = gathered_by_axis(counts[None, :], OWNERS_SUB, (0, 2, 1), 0)
    own_index = lax.axis_index(OWNERS_SUB)
    column = jnp.sum(jnp.where(shard_ids[None, :] == own_index, all_counts, 0), axis=1)
    received_position = place_column(column, capacity)
    shard_totals = jnp.sum(all_counts, axis=0)
    return (received_rows, received_score, received_position, shard_totals)


def solution(mesh):
    split = Mesh(
        mesh.devices.reshape(mesh.shape["groups"], 8, 2, mesh.shape["sub"]),
        ("groups", "owners_0", "owners_1", "sub"),
    )
    in_specs = (
        P(GROUPS_OWNERS_SUB, None),
        P(),
        P(GROUPS_OWNERS_SUB),
        P(),
        P(GROUPS_OWNERS_SUB, None),
    )
    out_specs = (
        P(GROUPS_OWNERS_SUB, None),
        P(GROUPS_OWNERS_SUB),
        P(GROUPS_OWNERS_SUB),
        P("groups"),
    )
    return jax.shard_map(
        on_device, mesh=split, in_specs=in_specs, out_specs=out_specs, check_vma=False
    )
```

profile of v0, /device:TPU:513, one launch (start us, length us, event | category | flops | bytes accessed | tf_op | source)
XLA Modules:
  0.0 127.5 jit_solution(17202897359766314484)
XLA Ops:
  0.6 1.0 select_reduce_fusion.2
  1.7 1.4 %multiply_reduce_fusion.1 = f32[512]{0:T(512)S(1)} fusion(bf16[512,768]{1,0:T(8,128)(2,1)} %param.5), kind=kLoop, calls=%fused_computation.9 | loop fusion | flops 1179136 | bytes 788480 | tf_op jit(solution)/shard_map/while/body/eval_jaxpr/reduce_sum | solution.py:53
  3.1 0.0 copy-start.1
  3.1 0.0 copy-start.3
  3.1 1.9 %multiply_reduce_fusion = f32[1000]{0:T(1024)S(1)} fusion(bf16[1000,768]{1,0:T(8,128)(2,1)} %param.6), kind=kLoop, calls=%fused_computation.2 | loop fusion | flops 2303000 | bytes 1540000 | tf_op jit(solution)/shard_map/reduce_sum | solution.py:76
  5.0 0.1 copy.17
  5.2 0.1 copy.16
  5.3 0.3 fusion.4
  5.7 0.3 convert_reduce_fusion
  6.1 1.2 select_reduce_fusion
  7.3 2.8 %scatter_custom_fusion = bf16[768,768]{1,0:T(8,128)(2,1)S(1)} fusion(s32[512]{0:T(512)S(1)} %bitcast.35, bf16[512,768]{1,0:T(8,128)(2,1)S(1)} %copy-done.1, bf16[]{:T(256)} %constant.21.clone.1), kind=kCustom, calls=%fused_computation.10 | custom fusion | bytes 1179650 | tf_op jit(solution)/shard_map/scatter | solution.py:101
  10.2 3.8 %scatter_custom_fusion.1 = bf16[768]{0:T(1024)(128)(2,1)S(1)} fusion(s32[512]{0:T(512)S(1)} %bitcast.36, bf16[512]{0:T(512)(128)(2,1)S(1)} %multiply_convert_fusion, bf16[]{:T(256)} %constant.21.clone.1), kind=kCustom, calls=%fused_computation.35 | custom fusion | bytes 1538 | tf_op jit(solution)/shard_map/scatter | solution.py:106
  13.9 0.3 reshape_reshape.9
  14.2 0.4 reshape.128
  14.7 1.6 %pad_maximum_fusion = bf16[128,6,769]{2,1,0:T(8,128)(2,1)} fusion(bf16[128,6,1]{2,1,0:T(8,128)(2,1)S(1)} %reshape_reshape.9, bf16[128,6,768]{2,1,0:T(8,128)(2,1)S(1)} %reshape.128), kind=kLoop, calls=%fused_computation.8 | loop fusion | flops 2362368 | bytes 2362368 | tf_op jit(solution)/shard_map/concatenate | solution.py:15
  16.3 27.8 %all-to-all-start = ((bf16[128,6,769]{2,1,0:T(8,128)(2,1)}), bf16[128,6,769]{2,1,0:T(8,128)(2,1)S(1)}, u32[]{:S(2)}, u32[]{:S(2)}) async-start(bf16[128,6,769]{2,1,0:T(8,128)(2,1)} %pad_maximum_fusion), calls=%async_computation | async-start | bytes 3670016 | tf_op jit(solution)/shard_map/all_to_all | solution.py:17
  44.1 48.6 %all-gather.3 = s32[8,1,128]{2,1,0:T(1,128)S(1)} all-gather(s32[1,1,128]{2,1,0:T(1,128)S(1)} %bitcast.34), channel_id=2, replica_groups=mesh['groups'=2,'owners_0'=8,'owners_1'=2,'sub'=8] {'owners_0'}, dimensions={0}, use_global_device_ids=true | all-gather | bytes 4608 | tf_op jit(solution)/shard_map/all_gather | solution.py:37
  92.7 18.9 %all-gather.1 = s32[64,1,128]{2,1,0:T(1,128)S(1)} all-gather(s32[8,1,128]{2,1,0:T(1,128)S(1)} %all-gather.3), channel_id=3, replica_groups=mesh['groups'=2,'owners_0'=8,'owners_1'=2,'sub'=8] {'sub'}, dimensions={0}, use_global_device_ids=true | all-gather | bytes 36864 | tf_op jit(solution)/shard_map/all_gather | solution.py:37
  111.6 11.2 %all-gather.2 = s32[16,8,1,128]{3,1,2,0:T(8,128)S(1)} all-gather(s32[8,8,1,128]{3,1,2,0:T(8,128)S(1)} %bitcast.28), channel_id=4, replica_groups=mesh['groups'=2,'owners_0'=8,'owners_1'=2,'sub'=8] {'owners_1'}, dimensions={0}, use_global_device_ids=true | all-gather | bytes 98304 | tf_op jit(solution)/shard_map/all_gather | solution.py:37
  122.8 0.5 reduce_sum.88
  123.4 0.3 select_reduce_fusion.3
  123.7 0.1 copy.21
  123.8 0.1 lt.27
  123.9 0.1 reshape.154
  124.0 0.2 reduce-window.20
  124.2 0.1 reduce.6
  124.3 0.1 add_select_fusion
  124.4 0.7 select_n.46
  125.1 0.1 slice.17
  125.2 1.2 reshape.129
  126.5 0.2 slice_reduce_fusion
  126.7 0.7 reshape_reshape.8
  (21 shorter events, 0.2 us)
Async XLA Ops:
  0.6 4.5 %copy-start.2 = (s32[512,1]{0,1:T(1,128)S(1)}, s32[512,1]{0,1:T(1,128)}, u32[]{:S(2)}) copy-start(s32[512,1]{0,1:T(1,128)} %param.9) | copy-start | bytes 6148
  3.1 3.0 %copy-start = (bf16[1000,768]{1,0:T(8,128)(2,1)S(1)}, bf16[1000,768]{1,0:T(8,128)(2,1)}, u32[]{:S(2)}) copy-start(bf16[1000,768]{1,0:T(8,128)(2,1)} %param.6) | copy-start | bytes 4608004
  3.1 3.0 %copy-start.1 = (bf16[512,768]{1,0:T(8,128)(2,1)S(1)}, bf16[512,768]{1,0:T(8,128)(2,1)}, u32[]{:S(2)}) copy-start(bf16[512,768]{1,0:T(8,128)(2,1)} %param.5) | copy-start | bytes 2359300
  3.1 3.0 %copy-start.3 = (s32[512]{0:T(512)S(1)}, s32[512]{0:T(512)}, u32[]{:S(2)}) copy-start(s32[512]{0:T(512)} %param.7) | copy-start | bytes 6148
  16.3 108.9 %all-to-all-start = ((bf16[128,6,769]{2,1,0:T(8,128)(2,1)}), bf16[128,6,769]{2,1,0:T(8,128)(2,1)S(1)}, u32[]{:S(2)}, u32[]{:S(2)}) async-start(bf16[128,6,769]{2,1,0:T(8,128)(2,1)} %pad_maximum_fusion), calls=%async_computation | async-start | bytes 3670016 | tf_op jit(solution)/shard_map/all_to_all | solution.py:17
where the time goes:
time: 128 us; the launch traced here: 127 us
  blocking collectives  78.8 us (62%)
  starting transfers between devices  27.8 us (22%)
  local copies, waits for them, and re-layouts  10.9 us (9%)
  other arithmetic  7.93 us (6%)
    all_gather x3, blocking collectives, stacked_from(): tiles = lax.all_gather(tiles, axes[k])  78.8 us
    all_to_all x1, starting transfers between devices, sent_together(): lax.all_to_all(both, axis, split_axis=split_dim, concat_axis=concat_dim,...  27.8 us
    scatter x1, local copies, waits for them, and re-layouts, on_device(): send_score = jnp.zeros((shard_count * capacity,), jnp.bfloat16).at[slot_i...  3.77 us
    scatter x1, local copies, waits for them, and re-layouts, on_device(): send_rows = jnp.zeros((shard_count * capacity, feature_width), jnp.bfloat...  2.83 us
  transfers between devices with their start and end apart: 1, of which 0 were waited for; matrix products, arithmetic and copies ran while one was open for 2% of the time, Pallas kernels for 0%

commit v1 on v0

v1 whole, which is shorter than its diff:
```python
import jax
import jax.numpy as jnp
from jax import lax
from jax.experimental import pallas as pl
from jax.experimental.pallas import tpu as pltpu
from jax.sharding import PartitionSpec as P

GROUP = ("owners", "sub")
ALL = ("groups", "owners", "sub")
LANES = 128
CHUNK = 256
F32 = jnp.float32
BF16 = jnp.bfloat16
NT = (((1,), (1,)), ((), ()))
NN = (((1,), (0,)), ((), ()))


def dot(a, b, dims=NN):
    return lax.dot_general(a, b, dims, preferred_element_type=F32)


def iota(shape, dim):
    return lax.broadcasted_iota(jnp.int32, shape, dim)


def mask(cond):
    return jnp.where(cond, 1.0, 0.0)


def pack_kernel(me, nearest, keep, target, emb_hbm, table_hbm, out, emb, table, sems):
    rows, width = emb.shape
    classes = table.shape[0]
    shards = out.shape[0] // 8
    cap = 3 * rows // (2 * shards)
    head = out.shape[1]
    get_emb = pltpu.make_async_copy(emb_hbm, emb, sems.at[0])
    get_table = pltpu.make_async_copy(table_hbm, table, sems.at[1])
    get_emb.start()
    get_table.start()

    near = nearest[...]
    dest = target[...]
    low = mask(iota((LANES, rows), 0) == (near & (LANES - 1))).astype(BF16)
    looked = dot(keep[...], low)
    kept = jnp.sum(jnp.where(iota(looked.shape, 0) == (near >> 7), looked, 0.0), axis=0, keepdims=True)
    named = jnp.where(iota((shards, rows), 0) == dest, kept, 0.0)
    named_b = named.astype(BF16)
    blk = LANES
    upper = mask((iota((blk, 2 * blk), 0) < iota((blk, 2 * blk), 1)) | (iota((blk, 2 * blk), 1) >= blk)).astype(BF16)
    before = jnp.zeros((shards, blk), F32)
    ranks = []
    for b in range(rows // blk):
        cut = slice(b * blk, (b + 1) * blk)
        both = dot(named_b[:, cut], upper)
        ranks.append(jnp.sum((both[:, :blk] + before) * named[:, cut], axis=0, keepdims=True))
        before = before + both[:, blk:]
    rank = jnp.concatenate(ranks, axis=1).astype(jnp.int32)
    counts = dot(jnp.ones((8, rows), BF16), named_b, NT)[:1]
    slot = jnp.where(kept > 0.5, 8 * dest + rank, -1)

    get_emb.wait()
    squares = []
    for b in range(rows // blk):
        part = emb[b * blk : (b + 1) * blk, :]
        gram = dot(part, part, NT)
        diag = iota((blk, blk), 0) == iota((blk, blk), 1)
        squares.append(jnp.sum(jnp.where(diag, gram, 0.0), axis=0, keepdims=True))
    inverse_row = lax.rsqrt(jnp.concatenate(squares, axis=1) + 1e-06)

    get_table.wait()
    given = jnp.zeros((1, rows), F32)
    others = jnp.full((1, rows), -jnp.inf, F32)
    for c in range(0, classes, CHUNK):
        size = min(CHUNK, classes - c)
        part = table[c : c + size, :]
        wide = part.astype(F32)
        inverse_class = lax.rsqrt(jnp.sum(wide * wide, axis=1, keepdims=True) + 1e-06)
        scaled = dot(part, emb[...], NT) * inverse_class
        match = (iota((size, rows), 0) + c) == near
        given = given + jnp.sum(jnp.where(match, scaled, 0.0), axis=0, keepdims=True)
        others = jnp.maximum(others, jnp.max(jnp.where(match, -1e30, scaled), axis=0, keepdims=True))
    score = (20.0 * (given - others) * inverse_row).astype(BF16).astype(F32)
    lane = (rank + cap * me[0]) & (LANES - 1)
    spread = jnp.where(iota((LANES, rows), 0) == lane, score, 0.0).astype(BF16)
    scores = dot(named_b, spread, NT)

    step = 256
    for g in range(0, 8 * shards, step):
        pick = mask((iota((step, rows), 0) + g) == slot).astype(BF16)
        main = dot(pick, emb[...])
        tail = main[:, head:]
        sub = iota((step, LANES), 0) & 7
        t0 = g // 8
        wide = (step // 8, 8, LANES)
        last = [
            pltpu.roll(tail, 2, 0),
            jnp.broadcast_to(counts, (step, LANES)),
            jnp.broadcast_to(scores[t0 : t0 + step // 8][:, None, :], wide).reshape(step, LANES),
            jnp.broadcast_to(before[t0 : t0 + step // 8][:, None, :], wide).reshape(step, LANES),
            jnp.zeros((step, LANES), F32),
        ]
        for k in range(head // LANES):
            piece = jnp.where(sub < 6, main[:, k * LANES : (k + 1) * LANES], last[k])
            piece = jnp.where(sub == 6, pltpu.roll(tail, 6 - k, 0), piece)
            out[g : g + step, k * LANES : (k + 1) * LANES] = piece.astype(BF16)


def unpack_kernel(got, out_rows, out_score, out_position, out_totals, extra):
    b = pl.program_id(0)
    m, width = out_rows.shape
    k = m // 6 * 8
    head = got.shape[1]
    row, col = iota((m, k), 0), iota((m, k), 1)
    source = (row * 10923) >> 16
    slot = row - 6 * source
    block = got[pl.ds(pl.multiple_of(b * k, k), k), :]
    pick = mask(col == 8 * source + slot).astype(BF16)
    out_rows[:, :head] = dot(pick, block).astype(BF16)
    tail = jnp.zeros((m, width - head), F32)
    for t in range(head // LANES):
        hit = (slot == t) & (col == 8 * source + 6)
        if t == 0:
            hit = hit | ((slot == 5) & (col == 8 * source + 7))
        tail = tail + dot(mask(hit).astype(BF16), block[:, t * LANES : (t + 1) * LANES])
    out_rows[:, head:] = tail.astype(BF16)

    @pl.when(b == 0)
    def _():
        shards = got.shape[0] // 8
        for t in range(3):
            extra[t] = got[:, (t + 1) * LANES : (t + 2) * LANES].astype(F32)
        counts, scores, own = (extra[t, pl.ds(7, shards, stride=8), :] for t in range(3))
        out_totals[...] = jnp.sum(counts, axis=0, keepdims=True).astype(jnp.int32)
        s = iota((shards, LANES), 0)
        for a in range(out_score.shape[0]):
            at = a * LANES + iota((1, LANES), 1)
            src = (at * 10923) >> 16
            j = at - 6 * src
            here = s == src
            score = jnp.sum(jnp.where(here, scores, 0.0), axis=0, keepdims=True)
            held = jnp.sum(jnp.where(here, own, 0.0), axis=0, keepdims=True).astype(jnp.int32)
            ahead = jnp.sum(jnp.where(s < src, own, 0.0), axis=0, keepdims=True).astype(jnp.int32)
            out_score[a : a + 1, :] = score.astype(BF16)
            out_position[a : a + 1, :] = jnp.where(j < held, ahead + j, -1)


def on_device(embeddings, class_table, nearest, keep_class, destination):
    shards = lax.axis_size(GROUP)
    rows, width = embeddings.shape
    cap = 3 * rows // (2 * shards)
    classes = class_table.shape[0]
    head = width - LANES
    me = lax.axis_index(GROUP).reshape(1)
    keep = jnp.pad(keep_class, (0, 8 * LANES - classes)).reshape(8, LANES).astype(BF16)
    vmem = pl.BlockSpec(memory_space=pltpu.VMEM)
    sent = pl.pallas_call(
        pack_kernel,
        in_specs=[
            pl.BlockSpec(memory_space=pltpu.SMEM),
            vmem,
            vmem,
            vmem,
            pl.BlockSpec(memory_space=pl.ANY),
            pl.BlockSpec(memory_space=pl.ANY),
        ],
        out_specs=vmem,
        out_shape=jax.ShapeDtypeStruct((8 * shards, head), BF16),
        scratch_shapes=[
            pltpu.VMEM((rows, width), BF16),
            pltpu.VMEM((classes, width), BF16),
            pltpu.SemaphoreType.DMA((2,)),
        ],
        name="pack",
    )(me, nearest.reshape(1, rows), keep, destination.reshape(1, rows), embeddings, class_table)
    got = lax.all_to_all(sent.reshape(shards, 8, head), GROUP, 0, 0, tiled=True)
    steps = 4
    slots = shards * cap
    received, score, position, totals = pl.pallas_call(
        unpack_kernel,
        grid=(steps,),
        in_specs=[vmem],
        out_specs=[
            pl.BlockSpec((slots // steps, width), lambda b: (b, 0)),
            pl.BlockSpec((slots // LANES, LANES), lambda b: (0, 0)),
            pl.BlockSpec((slots // LANES, LANES), lambda b: (0, 0)),
            pl.BlockSpec((1, shards), lambda b: (0, 0)),
        ],
        out_shape=[
            jax.ShapeDtypeStruct((slots, width), BF16),
            jax.ShapeDtypeStruct((slots // LANES, LANES), BF16),
            jax.ShapeDtypeStruct((slots // LANES, LANES), jnp.int32),
            jax.ShapeDtypeStruct((1, shards), jnp.int32),
        ],
        scratch_shapes=[pltpu.VMEM((3, 8 * shards, LANES), F32)],
        name="unpack",
    )(got.reshape(8 * shards, head))
    return received, score.reshape(slots), position.reshape(slots), totals.reshape(shards)


def solution(mesh):
    return jax.shard_map(
        on_device,
        mesh=mesh,
        in_specs=(P(ALL, None), P(), P(ALL), P(), P(ALL, None)),
        out_specs=(P(ALL, None), P(ALL), P(ALL), P("groups")),
        check_vma=False,
    )
```

time: 128 us -> 77.8 us (0.61)
  starting transfers between devices: 27.8 us -> 0 us
  blocking collectives: 78.8 us -> 65.1 us
  Pallas kernels: 0 us -> 10.5 us
  local copies, waits for them, and re-layouts: 10.9 us -> 0.58 us
  other arithmetic: 7.93 us -> 0.69 us
    all_gather x3 -> x0, blocking collectives: 78.8 us -> none  [stacked_from(): tiles = lax.all_gather(tiles, axes[k])]
    all_to_all x0 -> x1, blocking collectives: none -> 65.1 us  [on_device(): got = lax.all_to_all(sent.reshape(shards, 8, head), GROUP, 0, 0, tiled=True)]
    all_to_all x1 -> x0, starting transfers between devices: 27.8 us -> none  [sent_together(): lax.all_to_all(both, axis, split_axis=split_dim, concat_axis=concat_dim,...]
    pallas_call x0 -> x2, Pallas kernels: none -> 10.5 us  [the longest x1 6.13 us: on_device(): pl.pallas_call(pack_kernel, in_specs=[pl.BlockSpec(memory_space=pltpu.SME...]
    scatter x2 -> x0, local copies, waits for them, and re-layouts: 6.59 us -> none  [the longest x1 3.77 us: on_device(): send_score = jnp.zeros((shard_count * capacity,), jnp.bfloat16).at[slot_i...]
    reduce_sum x6 -> x0, other arithmetic: 5.49 us -> none  [the longest x1 1.91 us: on_device(): jnp.sum(class_float * class_float, axis=1) + 1e-06]
    reshape x2 -> x0, local copies, waits for them, and re-layouts: 1.67 us -> none  [the longest x1 1.24 us: on_device(): received_rows = got_rows.reshape(shard_count * capacity, feature_width)]
    concatenate x1 -> x0, other arithmetic: 1.61 us -> none  [sent_together(): both = jnp.concatenate(columns, axis=along)]
  transfers between devices with their start and end apart: 1 -> 0, of which waited for: 0 -> 0; matrix products, arithmetic and copies ran while one was open for 2% -> 0% of each run, Pallas kernels for 0% -> 0%
where the time goes in v1:
time: 77.8 us; the launch traced here: 77.5 us
  blocking collectives  65.1 us (84%)
  Pallas kernels  10.5 us (13%)
    all_to_all x1, blocking collectives, on_device(): got = lax.all_to_all(sent.reshape(shards, 8, head), GROUP, 0, 0, tiled=True)  65.1 us
    pallas_call x1, Pallas kernels, on_device(): pl.pallas_call(pack_kernel, in_specs=[pl.BlockSpec(memory_space=pltpu.SME...  6.13 us
    pallas_call x1, Pallas kernels, on_device(): pl.pallas_call(unpack_kernel, grid=(steps,), in_specs=[vmem], out_specs=[...  4.35 us

profile of v1, /device:TPU:513, one launch (start us, length us, event | category | flops | bytes accessed | tf_op | source)
XLA Modules:
  0.0 77.5 jit_solution(16879326265195411833)
XLA Ops:
  0.6 0.7 convert.4
  1.3 0.6 pad_bitcast_fusion.keep
  1.9 6.1 %pack.1 = bf16[1024,640]{1,0:T(8,128)(2,1)} custom-call(s32[1]{0:T(128)} %bitcast.me, s32[1,512]{1,0:T(1,128)} %bitcast.12, bf16[8,128]{1,0:T(8,128)(2,1)} %pad_bitcast_fusion.keep, s32[1,512]{1,0:T(1,128)} %bitcast.13, bf16[512,768]{1,0:T(8,128)(2,1)} %emb_hbm.1, bf16[1000,768]{1,0:T(8,128)(2,1)} %table_hbm.1), custom_call_target="tpu_custom_call" | custom-call | tf_op jit(solution)/shard_map/pack/pallas_call | solution.py:156
  8.0 65.1 %all_to_all.5 = bf16[128,8,640]{2,1,0:T(8,128)(2,1)} all-to-all(bf16[128,8,640]{2,1,0:T(8,128)(2,1)} %bitcast.10), channel_id=1, replica_groups=mesh['groups'=2,'owners'=16,'sub'=8] {'owners','sub'}, dimensions={0} | all-to-all | bytes 2621440 | tf_op jit(solution)/shard_map/all_to_all | solution.py:175
  73.2 4.3 %unpack.1 = (bf16[768,768]{1,0:T(8,128)(2,1)}, bf16[6,128]{1,0:T(8,128)(2,1)}, s32[6,128]{1,0:T(8,128)}, s32[1,128]{1,0:T(1,128)}) custom-call(bf16[1024,640]{1,0:T(8,128)(2,1)} %bitcast.11), custom_call_target="tpu_custom_call" | custom-call | tf_op jit(solution)/shard_map/unpack/pallas_call | solution.py:178

commit v2 on v1

v2 whole, which is shorter than its diff:
```python
import jax
import jax.numpy as jnp
from jax import lax
from jax.experimental import pallas as pl
from jax.experimental.pallas import tpu as pltpu
from jax.sharding import PartitionSpec as P

GROUP = ("owners", "sub")
ALL = ("groups", "owners", "sub")
LANES = 128
CHUNK = 256
CAP = 6
HALF = CAP // 2
F32 = jnp.float32
BF16 = jnp.bfloat16
NT = (((1,), (1,)), ((), ()))
NN = (((1,), (0,)), ((), ()))


def dot(a, b, dims=NN):
    return lax.dot_general(a, b, dims, preferred_element_type=F32)


def iota(shape, dim):
    return lax.broadcasted_iota(jnp.int32, shape, dim)


def mask(cond):
    return jnp.where(cond, 1.0, 0.0)


def sixth(x):
    return (x * 10923) >> 16


def pack_kernel(me, near_hbm, keep_hbm, dest_hbm, emb_hbm, table_hbm, out, near_v, keep_v, dest_v, emb, table, sems):
    rows, width = emb.shape
    classes = table.shape[0]
    shards = out.shape[0]
    moves = [
        pltpu.make_async_copy(a, b, sems.at[i])
        for i, (a, b) in enumerate(
            [(near_hbm, near_v), (keep_hbm, keep_v), (dest_hbm, dest_v), (emb_hbm, emb), (table_hbm, table)]
        )
    ]
    for move in moves:
        move.start()
    for move in moves[:3]:
        move.wait()

    near = near_v[...]
    dest = dest_v[...]
    full, spare = classes // LANES, classes % LANES
    known = [keep_v[:, i * LANES : (i + 1) * LANES] for i in range(full)]
    if spare:
        known.append(pltpu.roll(keep_v[:, classes - LANES :], spare, 1))
    known.extend([jnp.zeros((1, LANES), jnp.int32)] * (8 - len(known)))
    low = mask(iota((LANES, rows), 0) == (near & (LANES - 1))).astype(BF16)
    looked = dot(jnp.concatenate(known, axis=0).astype(BF16), low)
    kept = jnp.sum(jnp.where(iota(looked.shape, 0) == (near >> 7), looked, 0.0), axis=0, keepdims=True)
    named = jnp.where(iota((shards, rows), 0) == dest, kept, 0.0)
    named_b = named.astype(BF16)
    blk = LANES
    upper = mask((iota((blk, 2 * blk), 0) < iota((blk, 2 * blk), 1)) | (iota((blk, 2 * blk), 1) >= blk)).astype(BF16)
    before = jnp.zeros((shards, blk), F32)
    ranks = []
    for b in range(rows // blk):
        cut = slice(b * blk, (b + 1) * blk)
        both = dot(named_b[:, cut], upper)
        ranks.append(jnp.sum((both[:, :blk] + before) * named[:, cut], axis=0, keepdims=True))
        before = before + both[:, blk:]
    rank = jnp.concatenate(ranks, axis=1).astype(jnp.int32)
    counts = dot(jnp.ones((8, rows), BF16), named_b, NT)[:1]
    slot = jnp.where(kept > 0.5, CAP * dest + rank, -1)
    second = jnp.where(kept > 0.5, 2 * dest + 1, -1)

    moves[3].wait()
    at = 3 * iota((2 * shards, rows), 0)
    pick = jnp.concatenate([mask(at + j == slot).astype(BF16) for j in range(HALF)], axis=0)
    whole = dot(pick, emb[...]).astype(BF16)
    for j in range(HALF):
        piece = whole[2 * shards * j : 2 * shards * (j + 1)]
        out[:, :, j * width : (j + 1) * width] = piece.reshape(shards, 2, width)
    squares = []
    for b in range(rows // blk):
        part = emb[b * blk : (b + 1) * blk, :]
        gram = dot(part, part, NT)
        diag = iota((blk, blk), 0) == iota((blk, blk), 1)
        squares.append(jnp.sum(jnp.where(diag, gram, 0.0), axis=0, keepdims=True))
    inverse_row = lax.rsqrt(jnp.concatenate(squares, axis=1) + 1e-06)

    moves[4].wait()
    given = jnp.zeros((1, rows), F32)
    others = jnp.full((1, rows), -jnp.inf, F32)
    for c in range(0, classes, CHUNK):
        size = min(CHUNK, classes - c)
        part = table[c : c + size, :]
        wide = part.astype(F32)
        inverse_class = lax.rsqrt(jnp.sum(wide * wide, axis=1, keepdims=True) + 1e-06)
        scaled = dot(part, emb[...], NT) * inverse_class
        match = (iota((size, rows), 0) + c) == near
        given = given + jnp.sum(jnp.where(match, scaled, 0.0), axis=0, keepdims=True)
        others = jnp.maximum(others, jnp.max(jnp.where(match, -1e30, scaled), axis=0, keepdims=True))
    score = (20.0 * (given - others) * inverse_row).astype(BF16).astype(F32)
    lane = (rank + CAP * me[0]) & (LANES - 1)
    spread = jnp.where(iota((LANES, rows), 0) == lane, score, 0.0).astype(BF16)
    scores = dot(mask(iota((2 * shards, rows), 0) == second).astype(BF16), spread, NT)
    more = jnp.where((iota((2 * shards, LANES), 0) & 1) == 0, counts, scores).astype(BF16)
    out[:, :, HALF * width :] = more.reshape(shards, 2, LANES)


def unpack_kernel(me, got, rows_hbm, score_hbm, position_hbm, totals_hbm, buf, score_v, position_v, totals_v, extra, sems):
    slots, width = rows_hbm.shape
    shards = got.shape[0]
    steps = sems.shape[0] - 3
    m, q = slots // steps, 2 * shards // steps
    third = (iota((m, m), 0) * 21846) >> 16
    pick = mask(third + q * (iota((m, m), 0) - HALF * third) == iota((m, m), 1)).astype(BF16)
    moves = []

    def start(src, dst):
        move = pltpu.make_async_copy(src, dst, sems.at[len(moves)])
        move.start()
        moves.append(move)

    for b in range(steps):
        block = got[b * (q // 2) : (b + 1) * (q // 2), :, : HALF * width].reshape(q, HALF * width)
        block = jnp.concatenate([block[:, j * width : (j + 1) * width] for j in range(HALF)], axis=0)
        buf[b * m : (b + 1) * m, :] = dot(pick, block).astype(BF16)
        start(buf.at[b * m : (b + 1) * m, :], rows_hbm.at[b * m : (b + 1) * m, :])
        if b != steps - 2:
            continue
        extra[...] = got[:, :, HALF * width :].reshape(2 * shards, LANES).astype(F32)
        counts, scores = extra[pl.ds(0, shards, stride=2), :], extra[pl.ds(1, shards, stride=2), :]
        totals_v[...] = jnp.sum(counts, axis=0, keepdims=True).astype(jnp.int32)
        mine = iota((shards, LANES), 1) == me[0]
        own = jnp.sum(jnp.where(mine, counts, 0.0), axis=1, keepdims=True)
        s = iota((shards, LANES), 0)
        for a in range(slots // LANES):
            at = a * LANES + iota((1, LANES), 1)
            src = sixth(at)
            j = at - CAP * src
            here = s == src
            score = jnp.sum(jnp.where(here, scores, 0.0), axis=0, keepdims=True)
            held = jnp.sum(jnp.where(here, own, 0.0), axis=0, keepdims=True).astype(jnp.int32)
            ahead = jnp.sum(jnp.where(s < src, own, 0.0), axis=0, keepdims=True).astype(jnp.int32)
            score_v[a : a + 1, :] = score.astype(BF16)
            position_v[a : a + 1, :] = jnp.where(j < held, ahead + j, -1)
        start(score_v, score_hbm)
        start(position_v, position_hbm)
        start(totals_v, totals_hbm)
    for move in moves:
        move.wait()


def on_device(embeddings, class_table, nearest, keep_class, destination):
    shards = lax.axis_size(GROUP)
    rows, width = embeddings.shape
    classes = class_table.shape[0]
    chunk = HALF * width + LANES
    me = lax.axis_index(GROUP).reshape(1)
    vmem = pl.BlockSpec(memory_space=pltpu.VMEM)
    smem = pl.BlockSpec(memory_space=pltpu.SMEM)
    hbm = pl.BlockSpec(memory_space=pl.ANY)
    sent = pl.pallas_call(
        pack_kernel,
        in_specs=[smem, hbm, hbm, hbm, hbm, hbm],
        out_specs=vmem,
        out_shape=pltpu.VMEM((shards, 2, chunk), BF16),
        scratch_shapes=[
            pltpu.VMEM((1, rows), jnp.int32),
            pltpu.VMEM((1, classes), jnp.int32),
            pltpu.VMEM((1, rows), jnp.int32),
            pltpu.VMEM((rows, width), BF16),
            pltpu.VMEM((classes, width), BF16),
            pltpu.SemaphoreType.DMA((5,)),
        ],
        name="pack",
    )(me, nearest.reshape(1, rows), keep_class.reshape(1, classes), destination.reshape(1, rows), embeddings, class_table)
    got = lax.all_to_all(sent, GROUP, 0, 0, tiled=True)
    steps = 4
    slots = shards * CAP
    tall = slots // LANES
    received, score, position, totals = pl.pallas_call(
        unpack_kernel,
        in_specs=[smem, vmem],
        out_specs=[hbm, hbm, hbm, hbm],
        out_shape=[
            jax.ShapeDtypeStruct((slots, width), BF16),
            jax.ShapeDtypeStruct((tall, LANES), BF16),
            jax.ShapeDtypeStruct((tall, LANES), jnp.int32),
            jax.ShapeDtypeStruct((1, shards), jnp.int32),
        ],
        scratch_shapes=[
            pltpu.VMEM((slots, width), BF16),
            pltpu.VMEM((tall, LANES), BF16),
            pltpu.VMEM((tall, LANES), jnp.int32),
            pltpu.VMEM((1, shards), jnp.int32),
            pltpu.VMEM((2 * shards, LANES), F32),
            pltpu.SemaphoreType.DMA((steps + 3,)),
        ],
        name="unpack",
    )(me, pltpu.with_memory_space_constraint(got, pltpu.VMEM))
    return received, score.reshape(slots), position.reshape(slots), totals.reshape(shards)


def solution(mesh):
    return jax.shard_map(
        on_device,
        mesh=mesh,
        in_specs=(P(ALL, None), P(), P(ALL), P(), P(ALL, None)),
        out_specs=(P(ALL, None), P(ALL), P(ALL), P("groups")),
        check_vma=False,
    )
```

time: 77.8 us -> 68.2 us (0.88)
  Pallas kernels: 10.5 us -> 5.31 us
  blocking collectives: 65.1 us -> 62.1 us
    pallas_call x2, Pallas kernels: 10.5 us -> 5.31 us  [the longest x1 3.91 us: on_device(): pl.pallas_call(pack_kernel, in_specs=[smem, hbm, hbm, hbm, hbm, hbm], out...]
    all_to_all x1, blocking collectives: 65.1 us -> 62.1 us  [on_device(): got = lax.all_to_all(sent, GROUP, 0, 0, tiled=True)]
where the time goes in v2:
time: 68.2 us; the launch traced here: 68.1 us
  blocking collectives  62.1 us (91%)
  Pallas kernels  5.31 us (8%)
    all_to_all x1, blocking collectives, on_device(): got = lax.all_to_all(sent, GROUP, 0, 0, tiled=True)  62.1 us
    pallas_call x1, Pallas kernels, on_device(): pl.pallas_call(pack_kernel, in_specs=[smem, hbm, hbm, hbm, hbm, hbm], out...  3.91 us
    pallas_call x1, Pallas kernels, on_device(): pl.pallas_call(unpack_kernel, in_specs=[smem, vmem], out_specs=[hbm, hbm,...  1.4 us

profile of v2, /device:TPU:513, one launch (start us, length us, event | category | flops | bytes accessed | tf_op | source)
XLA Modules:
  0.0 68.1 jit_solution(4909955495884869708)
XLA Ops:
  0.6 3.9 %pack.1 = bf16[128,2,2432]{2,1,0:T(2,128)(2,1)S(1)} custom-call(s32[1]{0:T(128)} %bitcast.me, s32[1,512]{1,0:T(1,128)} %bitcast.8, s32[1,1000]{1,0:T(1,128)} %bitcast.7, s32[1,512]{1,0:T(1,128)} %bitcast.9, bf16[512,768]{1,0:T(8,128)(2,1)} %emb_hbm.1, bf16[1000,768]{1,0:T(8,128)(2,1)} %table_hbm.1), custom_call_target="tpu_custom_call" | custom-call | tf_op jit(solution)/shard_map/pack/pallas_call | solution.py:165
  4.6 62.1 %all_to_all.5.got = bf16[128,2,2432]{2,1,0:T(2,128)(2,1)S(1)} all-to-all(bf16[128,2,2432]{2,1,0:T(2,128)(2,1)S(1)} %pack.1), channel_id=1, replica_groups=mesh['groups'=2,'owners'=16,'sub'=8] {'owners','sub'}, dimensions={0} | all-to-all | bytes 2490368 | tf_op jit(solution)/shard_map/all_to_all | solution.py:180
  66.7 1.4 %unpack.1 = (bf16[768,768]{1,0:T(8,128)(2,1)}, bf16[6,128]{1,0:T(8,128)(2,1)}, s32[6,128]{1,0:T(8,128)}, s32[1,128]{1,0:T(1,128)}) custom-call(s32[1]{0:T(128)} %bitcast.me, bf16[128,2,2432]{2,1,0:T(2,128)(2,1)S(1)} %all_to_all.5.got), custom_call_target="tpu_custom_call" | custom-call | tf_op jit(solution)/shard_map/unpack/pallas_call | solution.py:184

commit v3 on v2

--- a/solution.py
+++ b/solution.py
@@ -1,12 +1,17 @@
+import functools
+
 import jax
 import jax.numpy as jnp
 from jax import lax
 from jax.experimental import pallas as pl
 from jax.experimental.pallas import tpu as pltpu
+from jax.sharding import Mesh
 from jax.sharding import PartitionSpec as P
 
-GROUP = ("owners", "sub")
-ALL = ("groups", "owners", "sub")
+CHIPS = ("x", "sub")
+GROUP = ("x", "core", "sub")
+ALL = ("groups", "x", "core", "sub")
+CORES = 2
 LANES = 128
 CHUNK = 256
 CAP = 6
@@ -33,7 +38,11 @@
     return (x * 10923) >> 16
 
 
-def pack_kernel(me, near_hbm, keep_hbm, dest_hbm, emb_hbm, table_hbm, out, near_v, keep_v, dest_v, emb, table, sems):
+def log2(n):
+    return n.bit_length() - 1
+
+
+def pack_kernel(subs, me, near_hbm, keep_hbm, dest_hbm, emb_hbm, table_hbm, out, near_v, keep_v, dest_v, emb, table, sems):
     rows, width = emb.shape
     classes = table.shape[0]
     shards = out.shape[0]
@@ -71,8 +80,11 @@
         before = before + both[:, blk:]
     rank = jnp.concatenate(ranks, axis=1).astype(jnp.int32)
     counts = dot(jnp.ones((8, rows), BF16), named_b, NT)[:1]
-    slot = jnp.where(kept > 0.5, CAP * dest + rank, -1)
-    second = jnp.where(kept > 0.5, 2 * dest + 1, -1)
+    core, y = (dest >> log2(subs)) & 1, dest & (subs - 1)
+    away = core ^ ((me[0] >> log2(subs)) & 1)
+    place = (dest - core * subs - y) + CORES * y + away
+    slot = jnp.where(kept > 0.5, CAP * place + rank, -1)
+    second = jnp.where(kept > 0.5, 2 * place + 1, -1)
 
     moves[3].wait()
     at = 3 * iota((2 * shards, rows), 0)
@@ -109,11 +121,14 @@
     out[:, :, HALF * width :] = more.reshape(shards, 2, LANES)
 
 
-def unpack_kernel(me, got, rows_hbm, score_hbm, position_hbm, totals_hbm, buf, score_v, position_v, totals_v, extra, sems):
-    slots, width = rows_hbm.shape
-    shards = got.shape[0]
-    steps = sems.shape[0] - 3
-    m, q = slots // steps, 2 * shards // steps
+def unpack_kernel(me, got, passed, rows_hbm, score_hbm, position_hbm, totals_hbm, buf, score_v, position_v, totals_v, extra, sems):
+    owners, _, deep, width = rows_hbm.shape
+    subs = deep // CAP
+    chips = passed.shape[0]
+    shards = CORES * chips
+    core = (me[0] >> log2(subs)) & 1
+    steps = 2
+    m, q = CAP * chips // steps, 2 * chips // steps
     third = (iota((m, m), 0) * 21846) >> 16
     pick = mask(third + q * (iota((m, m), 0) - HALF * third) == iota((m, m), 1)).astype(BF16)
     moves = []
@@ -123,20 +138,27 @@
         move.start()
         moves.append(move)
 
-    for b in range(steps):
-        block = got[b * (q // 2) : (b + 1) * (q // 2), :, : HALF * width].reshape(q, HALF * width)
+    for b in range(2 * steps):
+        at = slice(b % steps * (q // 2), (b % steps + 1) * (q // 2))
+        block = got[at, 0, :, : HALF * width] if b < steps else passed[at, :, : HALF * width]
+        block = block.reshape(q, HALF * width)
         block = jnp.concatenate([block[:, j * width : (j + 1) * width] for j in range(HALF)], axis=0)
-        buf[b * m : (b + 1) * m, :] = dot(pick, block).astype(BF16)
-        start(buf.at[b * m : (b + 1) * m, :], rows_hbm.at[b * m : (b + 1) * m, :])
-        if b != steps - 2:
+        part = owners // steps
+        buf[b * part : (b + 1) * part] = dot(pick, block).astype(BF16).reshape(part, deep, width)
+        where = core if b < steps else 1 - core
+        start(buf.at[b * part : (b + 1) * part], rows_hbm.at[b % steps * part : (b % steps + 1) * part, where])
+        if b != 2 * steps - 2:
             continue
-        extra[...] = got[:, :, HALF * width :].reshape(2 * shards, LANES).astype(F32)
+        extra[: 2 * chips] = got[:, 0, :, HALF * width :].reshape(2 * chips, LANES).astype(F32)
+        extra[2 * chips :] = passed[:, :, HALF * width :].reshape(2 * chips, LANES).astype(F32)
         counts, scores = extra[pl.ds(0, shards, stride=2), :], extra[pl.ds(1, shards, stride=2), :]
         totals_v[...] = jnp.sum(counts, axis=0, keepdims=True).astype(jnp.int32)
         mine = iota((shards, LANES), 1) == me[0]
         own = jnp.sum(jnp.where(mine, counts, 0.0), axis=1, keepdims=True)
-        s = iota((shards, LANES), 0)
-        for a in range(slots // LANES):
+        i = iota((shards, LANES), 0)
+        x, y = (i & (chips - 1)) >> log2(subs), i & (subs - 1)
+        s = (CORES * x + jnp.where(i < chips, core, 1 - core)) * subs + y
+        for a in range(CAP * shards // LANES):
             at = a * LANES + iota((1, LANES), 1)
             src = sixth(at)
             j = at - CAP * src
@@ -154,7 +176,7 @@
 
 
 def on_device(embeddings, class_table, nearest, keep_class, destination):
-    shards = lax.axis_size(GROUP)
+    shards, chips, owners, subs = (lax.axis_size(a) for a in (GROUP, CHIPS, "x", "sub"))
     rows, width = embeddings.shape
     classes = class_table.shape[0]
     chunk = HALF * width + LANES
@@ -163,7 +185,7 @@
     smem = pl.BlockSpec(memory_space=pltpu.SMEM)
     hbm = pl.BlockSpec(memory_space=pl.ANY)
     sent = pl.pallas_call(
-        pack_kernel,
+        functools.partial(pack_kernel, subs),
         in_specs=[smem, hbm, hbm, hbm, hbm, hbm],
         out_specs=vmem,
         out_shape=pltpu.VMEM((shards, 2, chunk), BF16),
@@ -177,37 +199,39 @@
         ],
         name="pack",
     )(me, nearest.reshape(1, rows), keep_class.reshape(1, classes), destination.reshape(1, rows), embeddings, class_table)
-    got = lax.all_to_all(sent, GROUP, 0, 0, tiled=True)
-    steps = 4
+    got = lax.all_to_all(sent.reshape(chips, CORES, 2, chunk), CHIPS, 0, 0, tiled=True)
+    passed = lax.ppermute(got[:, 1], "core", [(0, 1), (1, 0)])
     slots = shards * CAP
     tall = slots // LANES
     received, score, position, totals = pl.pallas_call(
         unpack_kernel,
-        in_specs=[smem, vmem],
+        in_specs=[smem, vmem, vmem],
         out_specs=[hbm, hbm, hbm, hbm],
         out_shape=[
-            jax.ShapeDtypeStruct((slots, width), BF16),
+            jax.ShapeDtypeStruct((owners, CORES, CAP * subs, width), BF16),
             jax.ShapeDtypeStruct((tall, LANES), BF16),
             jax.ShapeDtypeStruct((tall, LANES), jnp.int32),
             jax.ShapeDtypeStruct((1, shards), jnp.int32),
         ],
         scratch_shapes=[
-            pltpu.VMEM((slots, width), BF16),
+            pltpu.VMEM((CORES * owners, CAP * subs, width), BF16),
             pltpu.VMEM((tall, LANES), BF16),
             pltpu.VMEM((tall, LANES), jnp.int32),
             pltpu.VMEM((1, shards), jnp.int32),
             pltpu.VMEM((2 * shards, LANES), F32),
-            pltpu.SemaphoreType.DMA((steps + 3,)),
+            pltpu.SemaphoreType.DMA((7,)),
         ],
         name="unpack",
-    )(me, pltpu.with_memory_space_constraint(got, pltpu.VMEM))
-    return received, score.reshape(slots), position.reshape(slots), totals.reshape(shards)
+    )(me, *(pltpu.with_memory_space_constraint(a, pltpu.VMEM) for a in (got, passed)))
+    return received.reshape(slots, width), score.reshape(slots), position.reshape(slots), totals.reshape(shards)
 
 
 def solution(mesh):
+    groups, owners, subs = (mesh.shape[a] for a in ("groups", "owners", "sub"))
+    split = Mesh(mesh.devices.reshape(groups, owners // CORES, CORES, subs), ALL)
     return jax.shard_map(
         on_device,
-        mesh=mesh,
+        mesh=split,
         in_specs=(P(ALL, None), P(), P(ALL), P(), P(ALL, None)),
         out_specs=(P(ALL, None), P(ALL), P(ALL), P("groups")),
         check_vma=False,

time: 68.2 us -> 63.4 us (0.930)
  blocking collectives: 62.1 us -> 48.6 us
  starting transfers between devices: 0 us -> 6.53 us
  waiting for transfers between devices: 0 us -> 1.68 us
    all_to_all x1, blocking collectives: 62.1 us -> 48.6 us  [on_device(): lax.all_to_all(sent.reshape(chips, CORES, 2, chunk), CHIPS, 0, 0, tiled=T...]
    ppermute x0 -> x1, starting transfers between devices: none -> 6.53 us  [on_device(): passed = lax.ppermute(got[:, 1], 'core', [(0, 1), (1, 0)])]
    ppermute x0 -> x1, waiting for transfers between devices: none -> 1.68 us  [on_device(): passed = lax.ppermute(got[:, 1], 'core', [(0, 1), (1, 0)])]
  transfers between devices with their start and end apart: 0 -> 1, of which waited for: 0 -> 1; matrix products, arithmetic and copies ran while one was open for 0% -> 0% of each run, Pallas kernels for 0% -> 0%
where the time goes in v3:
time: 63.4 us; the launch traced here: 63.2 us
  blocking collectives  48.6 us (77%)
  starting transfers between devices  6.53 us (10%)
  Pallas kernels  5.3 us (8%)
  waiting for transfers between devices  1.68 us (3%)
  between operations  0.65 us (1%)
    all_to_all x1, blocking collectives, on_device(): lax.all_to_all(sent.reshape(chips, CORES, 2, chunk), CHIPS, 0, 0, tiled=T...  48.6 us
    ppermute x1, starting transfers between devices, on_device(): passed = lax.ppermute(got[:, 1], 'core', [(0, 1), (1, 0)])  6.53 us
    pallas_call x1, Pallas kernels, on_device(): pl.pallas_call(functools.partial(pack_kernel, subs), in_specs=[smem, hbm,...  3.89 us
    ppermute x1, waiting for transfers between devices, on_device(): passed = lax.ppermute(got[:, 1], 'core', [(0, 1), (1, 0)])  1.68 us
    pallas_call x1, Pallas kernels, on_device(): pl.pallas_call(unpack_kernel, in_specs=[smem, vmem, vmem], out_specs=[hbm...  1.41 us
  transfers between devices with their start and end apart: 1, of which 1 were waited for; matrix products, arithmetic and copies ran while one was open for 0% of the time, Pallas kernels for 0%

profile of v3, /device:TPU:513, one launch (start us, length us, event | category | flops | bytes accessed | tf_op | source)
XLA Modules:
  0.0 63.2 jit_solution(1140708165167033494)
XLA Ops:
  0.6 3.9 %pack.1 = bf16[128,2,2432]{2,1,0:T(2,128)(2,1)S(1)} custom-call(s32[1]{0:T(128)} %bitcast.me, s32[1,512]{1,0:T(1,128)} %bitcast.15, s32[1,1000]{1,0:T(1,128)} %bitcast.14, s32[1,512]{1,0:T(1,128)} %bitcast.16, bf16[512,768]{1,0:T(8,128)(2,1)} %emb_hbm.1, bf16[1000,768]{1,0:T(8,128)(2,1)} %table_hbm.1), custom_call_target="tpu_custom_call" | custom-call | tf_op jit(solution)/shard_map/pack/pallas_call | solution.py:187
  4.5 48.6 %all_to_all.5.got = bf16[64,2,2,2432]{3,2,1,0:T(2,128)(2,1)S(1)} all-to-all(bf16[64,2,2,2432]{3,2,1,0:T(2,128)(2,1)S(1)} %bitcast.13), channel_id=1, replica_groups=mesh['groups'=2,'x'=8,'core'=2,'sub'=8] {'x','sub'}, dimensions={0} | all-to-all | bytes 2490368 | tf_op jit(solution)/shard_map/all_to_all | solution.py:202
  53.1 0.4 slice_bitcast_fusion
  53.6 6.5 %collective-permute-start = (bf16[64,2,2432]{2,1,0:T(2,128)(2,1)S(1)}, bf16[64,2,2432]{2,1,0:T(2,128)(2,1)S(1)}, u32[]{:S(2)}, u32[]{:S(2)}) collective-permute-start(bf16[64,2,2432]{2,1,0:T(2,128)(2,1)S(1)} %slice_bitcast_fusion), channel_id=1, source_target_pairs={{0,8},{8,0},{1,9},{9,1},{2,10},{10,2},{3,11},{11,3},{4,12},{12,4},... | collective-permute-start | bytes 1867784 | tf_op jit(solution)/shard_map/ppermute | solution.py:203
  60.1 1.7 %collective-permute-done.passed = bf16[64,2,2432]{2,1,0:T(2,128)(2,1)S(1)} collective-permute-done((bf16[64,2,2432]{2,1,0:T(2,128)(2,1)S(1)}, bf16[64,2,2432]{2,1,0:T(2,128)(2,1)S(1)}, u32[]{:S(2)}, u32[]{:S(2)}) %collective-permute-start) | collective-permute-done | bytes 622624 | tf_op jit(solution)/shard_map/ppermute | solution.py:203
  61.8 1.4 %unpack.1 = (bf16[8,2,48,768]{3,2,1,0:T(8,128)(2,1)}, bf16[6,128]{1,0:T(8,128)(2,1)}, s32[6,128]{1,0:T(8,128)}, s32[1,128]{1,0:T(1,128)}) custom-call(s32[1]{0:T(128)} %bitcast.me, bf16[64,2,2,2432]{3,2,1,0:T(2,128)(2,1)S(1)} %all_to_all.5.got, bf16[64,2,2432]{2,1,0:T(2,128)(2,1)S(1)} %collective-permute-done.passed), custom_call_target="tpu_custom_call" | custom-call | tf_op jit(solution)/shard_map/unpack/pallas_call | solution.py:206
Async XLA Ops:
  53.6 8.2 %collective-permute-start = (bf16[64,2,2432]{2,1,0:T(2,128)(2,1)S(1)}, bf16[64,2,2432]{2,1,0:T(2,128)(2,1)S(1)}, u32[]{:S(2)}, u32[]{:S(2)}) collective-permute-start(bf16[64,2,2432]{2,1,0:T(2,128)(2,1)S(1)} %slice_bitcast_fusion), channel_id=1, source_target_pairs={{0,8},{8,0},{1,9},{9,1},{2,10},{10,2},{3,11},{11,3},{4,12},{12,4},... | collective-permute-start | bytes 1867784 | tf_op jit(solution)/shard_map/ppermute | solution.py:203

commit v4 on v3

v4 whole, which is shorter than its diff:
```python
import functools

import jax
import jax.numpy as jnp
from jax import lax
from jax.experimental import pallas as pl
from jax.experimental.pallas import tpu as pltpu
from jax.sharding import Mesh
from jax.sharding import PartitionSpec as P

CHIPS = ("x", "sub")
GROUP = ("x", "core", "sub")
ALL = ("groups", "x", "core", "sub")
CORES = 2
LANES = 128
CHUNK = 256
CAP = 6
HALF = CAP // 2
F32 = jnp.float32
BF16 = jnp.bfloat16
NT = (((1,), (1,)), ((), ()))
NN = (((1,), (0,)), ((), ()))


def dot(a, b, dims=NN):
    return lax.dot_general(a, b, dims, preferred_element_type=F32)


def iota(shape, dim):
    return lax.broadcasted_iota(jnp.int32, shape, dim)


def mask(cond):
    return jnp.where(cond, 1.0, 0.0)


def sixth(x):
    return (x * 10923) >> 16


def log2(n):
    return n.bit_length() - 1


def pack_kernel(subs, me, near_hbm, keep_hbm, dest_hbm, emb_hbm, table_hbm, out, near_v, keep_v, dest_v, emb, table, sems):
    rows, width = emb.shape
    classes = table.shape[0]
    chips = out.shape[0]
    shards = CORES * chips
    starts = range(0, classes, CHUNK)
    pairs = [(near_hbm, near_v), (keep_hbm, keep_v), (dest_hbm, dest_v)]
    for r in range(0, rows, rows):
        pairs.append((emb_hbm.at[r : r + rows], emb.at[r : r + rows]))
    for c in starts:
        size = min(CHUNK, classes - c)
        pairs.append((table_hbm.at[c : c + size], table.at[c : c + size]))
    moves = [pltpu.make_async_copy(a, b, sems.at[i]) for i, (a, b) in enumerate(pairs)]
    for move in moves:
        move.start()
    for move in moves[:3]:
        move.wait()

    near = near_v[...]
    dest = dest_v[...]
    full, spare = classes // LANES, classes % LANES
    known = [keep_v[:, i * LANES : (i + 1) * LANES] for i in range(full)]
    if spare:
        known.append(pltpu.roll(keep_v[:, classes - LANES :], spare, 1))
    known.extend([jnp.zeros((1, LANES), jnp.int32)] * (8 - len(known)))
    low = mask(iota((LANES, rows), 0) == (near & (LANES - 1))).astype(BF16)
    looked = dot(jnp.concatenate(known, axis=0).astype(BF16), low)
    kept = jnp.sum(jnp.where(iota(looked.shape, 0) == (near >> 7), looked, 0.0), axis=0, keepdims=True)
    named = jnp.where(iota((shards, rows), 0) == dest, kept, 0.0)
    named_b = named.astype(BF16)
    blk = LANES
    upper = mask((iota((blk, 2 * blk), 0) < iota((blk, 2 * blk), 1)) | (iota((blk, 2 * blk), 1) >= blk)).astype(BF16)
    before = jnp.zeros((shards, blk), F32)
    ranks = []
    for b in range(rows // blk):
        cut = slice(b * blk, (b + 1) * blk)
        both = dot(named_b[:, cut], upper)
        ranks.append(jnp.sum((both[:, :blk] + before) * named[:, cut], axis=0, keepdims=True))
        before = before + both[:, blk:]
    rank = jnp.concatenate(ranks, axis=1).astype(jnp.int32)
    counts = dot(jnp.ones((8, rows), BF16), named_b, NT)[:1]
    core, y = (dest >> log2(subs)) & 1, dest & (subs - 1)
    away = core ^ ((me[0] >> log2(subs)) & 1)
    chip = ((dest - core * subs - y) >> 1) + y
    slot = jnp.where(kept > 0.5, CAP * (away * chips + chip) + rank, -1)
    second = jnp.where(kept > 0.5, 2 * chip + 1, -1)
    at = 3 * iota((2 * shards, rows), 0)

    def place(j):
        picked = dot(mask(at == slot - j).astype(BF16), emb[...]).astype(BF16)
        for k in range(CORES):
            piece = picked[2 * chips * k : 2 * chips * (k + 1)].reshape(chips, 2, width)
            out[:, :, (HALF * k + j) * width : (HALF * k + j + 1) * width] = piece

    def class_scale(c):
        wide = table[c : min(c + CHUNK, classes), :].astype(F32)
        return lax.rsqrt(jnp.sum(wide * wide, axis=1, keepdims=True) + 1e-06)

    for move in moves[3:4]:
        move.wait()
    place(0)
    place(1)
    squares = []
    for b in range(rows // blk):
        part = emb[b * blk : (b + 1) * blk, :]
        gram = dot(part, part, NT)
        diag = iota((blk, blk), 0) == iota((blk, blk), 1)
        squares.append(jnp.sum(jnp.where(diag, gram, 0.0), axis=0, keepdims=True))
    inverse_row = lax.rsqrt(jnp.concatenate(squares, axis=1) + 1e-06)
    for move in moves[4:]:
        move.wait()
    inverse_class = {}
    given = jnp.zeros((1, rows), F32)
    others = jnp.full((1, rows), -jnp.inf, F32)
    for c in starts:
        size = min(CHUNK, classes - c)
        inverse_class[c] = class_scale(c)
        scaled = dot(table[c : c + size, :], emb[...], NT) * inverse_class[c]
        match = iota((size, rows), 0) == near - c
        given = given + jnp.sum(jnp.where(match, scaled, 0.0), axis=0, keepdims=True)
        others = jnp.maximum(others, jnp.max(jnp.where(match, -1e30, scaled), axis=0, keepdims=True))
    score = (20.0 * (given - others) * inverse_row).astype(BF16).astype(F32)
    lane = (rank + CAP * me[0] + LANES // CORES * away) & (LANES - 1)
    spread = jnp.where(iota((LANES, rows), 0) == lane, score, 0.0).astype(BF16)
    place(2)
    scores = dot(mask(iota((2 * chips, rows), 0) == second).astype(BF16), spread, NT)
    more = jnp.where((iota((2 * chips, LANES), 0) & 1) == 0, counts, scores).astype(BF16)
    out[:, :, CAP * width :] = more.reshape(chips, 2, LANES)


def unpack_half(src, side, buf, rows_hbm, sems, between=None):
    owners, _, deep, width = rows_hbm.shape
    chips = owners * deep // CAP
    steps = sems.shape[0]
    m, q, part = CAP * chips // steps, 2 * chips // steps, owners // steps
    third = (iota((m, m), 0) * 21846) >> 16
    pick = mask(third + q * (iota((m, m), 0) - HALF * third) == iota((m, m), 1)).astype(BF16)
    moves = []
    for b in range(steps):
        if between and b == steps - 1:
            between()
        block = src(b * (q // 2), (b + 1) * (q // 2)).reshape(q, HALF * width)
        block = jnp.concatenate([block[:, j * width : (j + 1) * width] for j in range(HALF)], axis=0)
        cut = slice(b * part, (b + 1) * part)
        buf[cut] = dot(pick, block).astype(BF16).reshape(part, deep, width)
        move = pltpu.make_async_copy(buf.at[cut], rows_hbm.at[cut, side], sems.at[b])
        move.start()
        moves.append(move)
    return moves


def own_kernel(me, got, rows_hbm, buf, sems):
    subs, width = rows_hbm.shape[2] // CAP, rows_hbm.shape[3]
    core = (me[0] >> log2(subs)) & 1
    for move in unpack_half(lambda a, b: got[a:b, :, : HALF * width], core, buf, rows_hbm, sems):
        move.wait()


def passed_kernel(
    me, got, passed, own_rows, rows_hbm, score_hbm, position_hbm, totals_hbm, buf, score_v, position_v, totals_v, extra, sems, late
):
    del own_rows
    subs, width = rows_hbm.shape[2] // CAP, rows_hbm.shape[3]
    chips = passed.shape[0]
    shards = CORES * chips
    core = (me[0] >> log2(subs)) & 1
    results = [(score_v, score_hbm), (position_v, position_hbm), (totals_v, totals_hbm)]
    small = [pltpu.make_async_copy(a, b, late.at[i]) for i, (a, b) in enumerate(results)]

    def between():
        extra[: 2 * chips] = got[:, :, CAP * width :].reshape(2 * chips, LANES).astype(F32)
        extra[2 * chips :] = passed[:, :, HALF * width :].reshape(2 * chips, LANES).astype(F32)
        counts, scores = extra[pl.ds(0, shards, stride=2), :], extra[pl.ds(1, shards, stride=2), :]
        scores = jnp.concatenate([scores[:chips], pltpu.roll(scores[chips:], LANES // CORES, 1)], axis=0)
        totals_v[...] = jnp.sum(counts, axis=0, keepdims=True).astype(jnp.int32)
        lane = iota((shards, LANES), 1) == me[0]
        own = jnp.sum(jnp.where(lane, counts, 0.0), axis=1, keepdims=True)
        i = iota((shards, LANES), 0)
        x, y = (i & (chips - 1)) >> log2(subs), i & (subs - 1)
        s = (CORES * x + jnp.where(i < chips, core, 1 - core)) * subs + y
        for a in range(CAP * shards // LANES):
            at = a * LANES + iota((1, LANES), 1)
            src = sixth(at)
            j = at - CAP * src
            here = s == src
            score = jnp.sum(jnp.where(here, scores, 0.0), axis=0, keepdims=True)
            held = jnp.sum(jnp.where(here, own, 0.0), axis=0, keepdims=True).astype(jnp.int32)
            ahead = jnp.sum(jnp.where(s < src, own, 0.0), axis=0, keepdims=True).astype(jnp.int32)
            score_v[a : a + 1, :] = score.astype(BF16)
            position_v[a : a + 1, :] = jnp.where(j < held, ahead + j, -1)
        for move in small:
            move.start()

    moves = unpack_half(lambda a, b: passed[a:b, :, : HALF * width], 1 - core, buf, rows_hbm, sems, between)
    for move in moves + small:
        move.wait()


def on_device(embeddings, class_table, nearest, keep_class, destination):
    shards, chips, owners, subs = (lax.axis_size(a) for a in (GROUP, CHIPS, "x", "sub"))
    rows, width = embeddings.shape
    classes = class_table.shape[0]
    chunk = CAP * width + LANES
    me = lax.axis_index(GROUP).reshape(1)
    vmem = pl.BlockSpec(memory_space=pltpu.VMEM)
    smem = pl.BlockSpec(memory_space=pltpu.SMEM)
    hbm = pl.BlockSpec(memory_space=pl.ANY)
    sent = pl.pallas_call(
        functools.partial(pack_kernel, subs),
        in_specs=[smem, hbm, hbm, hbm, hbm, hbm],
        out_specs=vmem,
        out_shape=pltpu.VMEM((chips, 2, chunk), BF16),
        scratch_shapes=[
            pltpu.VMEM((1, rows), jnp.int32),
            pltpu.VMEM((1, classes), jnp.int32),
            pltpu.VMEM((1, rows), jnp.int32),
            pltpu.VMEM((rows, width), BF16),
            pltpu.VMEM((classes, width), BF16),
            pltpu.SemaphoreType.DMA((4 + pl.cdiv(classes, CHUNK),)),
        ],
        name="pack",
    )(me, nearest.reshape(1, rows), keep_class.reshape(1, classes), destination.reshape(1, rows), embeddings, class_table)
    got = lax.all_to_all(sent, CHIPS, 0, 0, tiled=True)
    passed = lax.ppermute(got[:, :, HALF * width :], "core", [(0, 1), (1, 0)])
    slots = shards * CAP
    tall = slots // LANES
    rows_shape = jax.ShapeDtypeStruct((owners, CORES, CAP * subs, width), BF16)
    buf = pltpu.VMEM((owners, CAP * subs, width), BF16)
    got = pltpu.with_memory_space_constraint(got, pltpu.VMEM)
    own_rows = pl.pallas_call(
        own_kernel,
        in_specs=[smem, vmem],
        out_specs=hbm,
        out_shape=rows_shape,
        scratch_shapes=[buf, pltpu.SemaphoreType.DMA((2,))],
        name="own",
    )(me, got)
    received, score, position, totals = pl.pallas_call(
        passed_kernel,
        in_specs=[smem, vmem, vmem, hbm],
        out_specs=[hbm, hbm, hbm, hbm],
        out_shape=[
            rows_shape,
            jax.ShapeDtypeStruct((tall, LANES), BF16),
            jax.ShapeDtypeStruct((tall, LANES), jnp.int32),
            jax.ShapeDtypeStruct((1, shards), jnp.int32),
        ],
        scratch_shapes=[
            buf,
            pltpu.VMEM((tall, LANES), BF16),
            pltpu.VMEM((tall, LANES), jnp.int32),
            pltpu.VMEM((1, shards), jnp.int32),
            pltpu.VMEM((2 * shards, LANES), F32),
            pltpu.SemaphoreType.DMA((2,)),
            pltpu.SemaphoreType.DMA((3,)),
        ],
        input_output_aliases={3: 0},
        name="passed",
    )(me, got, pltpu.with_memory_space_constraint(passed, pltpu.VMEM), own_rows)
    return received.reshape(slots, width), score.reshape(slots), position.reshape(slots), totals.reshape(shards)


def solution(mesh):
    groups, owners, subs = (mesh.shape[a] for a in ("groups", "owners", "sub"))
    split = Mesh(mesh.devices.reshape(groups, owners // CORES, CORES, subs), ALL)
    return jax.shard_map(
        on_device,
        mesh=split,
        in_specs=(P(ALL, None), P(), P(ALL), P(), P(ALL, None)),
        out_specs=(P(ALL, None), P(ALL), P(ALL), P("groups")),
        check_vma=False,
    )
```

time: 63.4 us -> 62.5 us (0.986)
  waiting for transfers between devices: 1.68 us -> 0.53 us
  Pallas kernels: 5.3 us -> 6.18 us
  blocking collectives: 48.6 us -> 47.8 us
    ppermute x1, waiting for transfers between devices: 1.68 us -> 0.53 us  [on_device(): passed = lax.ppermute(got[:, :, HALF * width:], 'core', [(0, 1), (1, 0)])]
    pallas_call x1 -> x2, Pallas kernels: 1.41 us -> 2.38 us  [the longest x1 1.24 us: on_device(): pl.pallas_call(passed_kernel, in_specs=[smem, vmem, vmem, hbm], out_specs...]
    all_to_all x1, blocking collectives: 48.6 us -> 47.8 us  [on_device(): got = lax.all_to_all(sent, CHIPS, 0, 0, tiled=True)]
  transfers between devices with their start and end apart: 1 -> 1, of which waited for: 1 -> 1; matrix products, arithmetic and copies ran while one was open for 0% -> 0% of each run, Pallas kernels for 0% -> 2%
where the time goes in v4:
time: 62.5 us; the launch traced here: 62.3 us
  blocking collectives  47.8 us (76%)
  starting transfers between devices  6.73 us (11%)
  Pallas kernels  6.18 us (10%)
  between operations  0.66 us (1%)
    all_to_all x1, blocking collectives, on_device(): got = lax.all_to_all(sent, CHIPS, 0, 0, tiled=True)  47.8 us
    ppermute x1, starting transfers between devices, on_device(): passed = lax.ppermute(got[:, :, HALF * width:], 'core', [(0, 1), (1, 0)])  6.73 us
    pallas_call x1, Pallas kernels, on_device(): pl.pallas_call(functools.partial(pack_kernel, subs), in_specs=[smem, hbm,...  3.8 us
  transfers between devices with their start and end apart: 1, of which 1 were waited for; matrix products, arithmetic and copies ran while one was open for 0% of the time, Pallas kernels for 2%

profile of v4, /device:TPU:513, one launch (start us, length us, event | category | flops | bytes accessed | tf_op | source)
XLA Modules:
  0.0 62.3 jit_solution(6754288736228194302)
XLA Ops:
  0.6 3.8 %pack.1 = bf16[64,2,4736]{2,1,0:T(2,128)(2,1)S(1)} custom-call(s32[1]{0:T(128)} %bitcast.me, s32[1,512]{1,0:T(1,128)} %bitcast.10, s32[1,1000]{1,0:T(1,128)} %bitcast.9, s32[1,512]{1,0:T(1,128)} %bitcast.11, bf16[512,768]{1,0:T(8,128)(2,1)} %emb_hbm.1, bf16[1000,768]{1,0:T(8,128)(2,1)} %table_hbm.1), custom_call_target="tpu_custom_call" | custom-call | tf_op jit(solution)/shard_map/pack/pallas_call | solution.py:212
  4.4 47.8 %all_to_all.5.got = bf16[64,2,4736]{2,1,0:T(2,128)(2,1)S(1)} all-to-all(bf16[64,2,4736]{2,1,0:T(2,128)(2,1)S(1)} %pack.1), channel_id=1, replica_groups=mesh['groups'=2,'x'=8,'core'=2,'sub'=8] {'x','sub'}, dimensions={0} | all-to-all | bytes 2424832 | tf_op jit(solution)/shard_map/all_to_all | solution.py:227
  52.2 0.4 slice.4
  52.7 6.7 %collective-permute-start = (bf16[64,2,2432]{2,1,0:T(2,128)(2,1)S(1)}, bf16[64,2,2432]{2,1,0:T(2,128)(2,1)S(1)}, u32[]{:S(2)}, u32[]{:S(2)}) collective-permute-start(bf16[64,2,2432]{2,1,0:T(2,128)(2,1)S(1)} %slice.4), channel_id=1, source_target_pairs={{0,8},{8,0},{1,9},{9,1},{2,10},{10,2},{3,11},{11,3},{4,12},{12,4},... | collective-permute-start | bytes 1867784 | tf_op jit(solution)/shard_map/ppermute | solution.py:228
  59.4 1.1 %own.1.own_rows = bf16[8,2,48,768]{3,2,1,0:T(8,128)(2,1)} custom-call(s32[1]{0:T(128)} %bitcast.me, bf16[64,2,4736]{2,1,0:T(2,128)(2,1)S(1)} %all_to_all.5.got), custom_call_target="tpu_custom_call" | custom-call | tf_op jit(solution)/shard_map/own/pallas_call | solution.py:234
  60.5 0.5 collective-permute-done.passed
  61.1 1.2 %passed.1 = (bf16[8,2,48,768]{3,2,1,0:T(8,128)(2,1)}, bf16[6,128]{1,0:T(8,128)(2,1)}, s32[6,128]{1,0:T(8,128)}, s32[1,128]{1,0:T(1,128)}) custom-call(s32[1]{0:T(128)} %bitcast.me, bf16[64,2,4736]{2,1,0:T(2,128)(2,1)S(1)} %all_to_all.5.got, bf16[64,2,2432]{2,1,0:T(2,128)(2,1)S(1)} %collective-permute-done.passed, ...), custom_call_target="tpu_custom_call", output_to_operand_aliasing={{0}: (3, {})} | custom-call | tf_op jit(solution)/shard_map/passed/pallas_call | solution.py:242
Async XLA Ops:
  52.7 8.4 %collective-permute-start = (bf16[64,2,2432]{2,1,0:T(2,128)(2,1)S(1)}, bf16[64,2,2432]{2,1,0:T(2,128)(2,1)S(1)}, u32[]{:S(2)}, u32[]{:S(2)}) collective-permute-start(bf16[64,2,2432]{2,1,0:T(2,128)(2,1)S(1)} %slice.4), channel_id=1, source_target_pairs={{0,8},{8,0},{1,9},{9,1},{2,10},{10,2},{3,11},{11,3},{4,12},{12,4},... | collective-permute-start | bytes 1867784 | tf_op jit(solution)/shard_map/ppermute | solution.py:228

commit v5 on v4

--- a/solution.py
+++ b/solution.py
@@ -13,7 +13,7 @@
 ALL = ("groups", "x", "core", "sub")
 CORES = 2
 LANES = 128
-CHUNK = 256
+CHUNK = 1024
 CAP = 6
 HALF = CAP // 2
 F32 = jnp.float32
@@ -153,6 +153,13 @@
     return moves
 
 
+def part_kernel(got, out):
+    chips, _, chunk = out.shape
+    for at in range(0, chunk, LANES):
+        skip = got.shape[2] - chunk + at
+        out[:, :, at : at + LANES] = got[:, :, skip : skip + LANES].reshape(2 * chips, LANES).reshape(chips, 2, LANES)
+
+
 def own_kernel(me, got, rows_hbm, buf, sems):
     subs, width = rows_hbm.shape[2] // CAP, rows_hbm.shape[3]
     core = (me[0] >> log2(subs)) & 1
@@ -225,12 +232,19 @@
         name="pack",
     )(me, nearest.reshape(1, rows), keep_class.reshape(1, classes), destination.reshape(1, rows), embeddings, class_table)
     got = lax.all_to_all(sent, CHIPS, 0, 0, tiled=True)
-    passed = lax.ppermute(got[:, :, HALF * width :], "core", [(0, 1), (1, 0)])
+    got = pltpu.with_memory_space_constraint(got, pltpu.VMEM)
+    passed = pl.pallas_call(
+        part_kernel,
+        in_specs=[vmem],
+        out_specs=vmem,
+        out_shape=pltpu.VMEM((chips, 2, HALF * width + LANES), BF16),
+        name="part",
+    )(got)
+    passed = lax.ppermute(passed, "core", [(0, 1), (1, 0)])
     slots = shards * CAP
     tall = slots // LANES
     rows_shape = jax.ShapeDtypeStruct((owners, CORES, CAP * subs, width), BF16)
     buf = pltpu.VMEM((owners, CAP * subs, width), BF16)
-    got = pltpu.with_memory_space_constraint(got, pltpu.VMEM)
     own_rows = pl.pallas_call(
         own_kernel,
         in_specs=[smem, vmem],

time: 62.5 us -> 62.1 us (level)
  no operation moved by 1% of the time
where the time goes in v5:
time: 62.1 us; the launch traced here: 61.9 us
  blocking collectives  47.8 us (77%)
  starting transfers between devices  6.7 us (11%)
  Pallas kernels  6.2 us (10%)
  between operations  0.66 us (1%)
    all_to_all x1, blocking collectives, on_device(): got = lax.all_to_all(sent, CHIPS, 0, 0, tiled=True)  47.8 us
    ppermute x1, starting transfers between devices, on_device(): passed = lax.ppermute(passed, 'core', [(0, 1), (1, 0)])  6.7 us
    pallas_call x1, Pallas kernels, on_device(): pl.pallas_call(functools.partial(pack_kernel, subs), in_specs=[smem, hbm,...  3.74 us
  transfers between devices with their start and end apart: 1, of which 1 were waited for; matrix products, arithmetic and copies ran while one was open for 0% of the time, Pallas kernels for 2%

profile of v5, /device:TPU:513, one launch (start us, length us, event | category | flops | bytes accessed | tf_op | source)
XLA Modules:
  0.0 61.9 jit_solution(1597441225501164351)
XLA Ops:
  0.6 3.7 %pack.1 = bf16[64,2,4736]{2,1,0:T(2,128)(2,1)S(1)} custom-call(s32[1]{0:T(128)} %bitcast.me, s32[1,512]{1,0:T(1,128)} %bitcast.10, s32[1,1000]{1,0:T(1,128)} %bitcast.9, s32[1,512]{1,0:T(1,128)} %bitcast.11, bf16[512,768]{1,0:T(8,128)(2,1)} %emb_hbm.1, bf16[1000,768]{1,0:T(8,128)(2,1)} %table_hbm.1), custom_call_target="tpu_custom_call" | custom-call | tf_op jit(solution)/shard_map/pack/pallas_call | solution.py:219
  4.4 47.8 %all_to_all.5.got = bf16[64,2,4736]{2,1,0:T(2,128)(2,1)S(1)} all-to-all(bf16[64,2,4736]{2,1,0:T(2,128)(2,1)S(1)} %pack.1), channel_id=1, replica_groups=mesh['groups'=2,'x'=8,'core'=2,'sub'=8] {'x','sub'}, dimensions={0} | all-to-all | bytes 2424832 | tf_op jit(solution)/shard_map/all_to_all | solution.py:234
  52.2 0.1 part.1
  52.3 6.7 %collective-permute-start = (bf16[64,2,2432]{2,1,0:T(2,128)(2,1)S(1)}, bf16[64,2,2432]{2,1,0:T(2,128)(2,1)S(1)}, u32[]{:S(2)}, u32[]{:S(2)}) collective-permute-start(bf16[64,2,2432]{2,1,0:T(2,128)(2,1)S(1)} %part.1), channel_id=1, source_target_pairs={{0,8},{8,0},{1,9},{9,1},{2,10},{10,2},{3,11},{11,3},{4,12},{12,4},... | collective-permute-start | bytes 1867784 | tf_op jit(solution)/shard_map/ppermute | solution.py:243
  59.0 1.1 %own.1.own_rows = bf16[8,2,48,768]{3,2,1,0:T(8,128)(2,1)} custom-call(s32[1]{0:T(128)} %bitcast.me, bf16[64,2,4736]{2,1,0:T(2,128)(2,1)S(1)} %all_to_all.5.got), custom_call_target="tpu_custom_call" | custom-call | tf_op jit(solution)/shard_map/own/pallas_call | solution.py:248
  60.1 0.5 collective-permute-done.passed
  60.7 1.2 %passed.1 = (bf16[8,2,48,768]{3,2,1,0:T(8,128)(2,1)}, bf16[6,128]{1,0:T(8,128)(2,1)}, s32[6,128]{1,0:T(8,128)}, s32[1,128]{1,0:T(1,128)}) custom-call(s32[1]{0:T(128)} %bitcast.me, bf16[64,2,4736]{2,1,0:T(2,128)(2,1)S(1)} %all_to_all.5.got, bf16[64,2,2432]{2,1,0:T(2,128)(2,1)S(1)} %collective-permute-done.passed, ...), custom_call_target="tpu_custom_call", output_to_operand_aliasing={{0}: (3, {})} | custom-call | tf_op jit(solution)/shard_map/passed/pallas_call | solution.py:256
Async XLA Ops:
  52.3 8.4 %collective-permute-start = (bf16[64,2,2432]{2,1,0:T(2,128)(2,1)S(1)}, bf16[64,2,2432]{2,1,0:T(2,128)(2,1)S(1)}, u32[]{:S(2)}, u32[]{:S(2)}) collective-permute-start(bf16[64,2,2432]{2,1,0:T(2,128)(2,1)S(1)} %part.1), channel_id=1, source_target_pairs={{0,8},{8,0},{1,9},{9,1},{2,10},{10,2},{3,11},{11,3},{4,12},{12,4},... | collective-permute-start | bytes 1867784 | tf_op jit(solution)/shard_map/ppermute | solution.py:243

commit v6 on v5

--- a/solution.py
+++ b/solution.py
@@ -113,16 +113,21 @@
     inverse_row = lax.rsqrt(jnp.concatenate(squares, axis=1) + 1e-06)
     for move in moves[4:]:
         move.wait()
-    inverse_class = {}
-    given = jnp.zeros((1, rows), F32)
-    others = jnp.full((1, rows), -jnp.inf, F32)
-    for c in starts:
-        size = min(CHUNK, classes - c)
-        inverse_class[c] = class_scale(c)
-        scaled = dot(table[c : c + size, :], emb[...], NT) * inverse_class[c]
-        match = iota((size, rows), 0) == near - c
-        given = given + jnp.sum(jnp.where(match, scaled, 0.0), axis=0, keepdims=True)
-        others = jnp.maximum(others, jnp.max(jnp.where(match, -1e30, scaled), axis=0, keepdims=True))
+    scale = [class_scale(c) for c in range(0, classes, 1024)]
+    given, others = [], []
+    for r in range(0, rows, 256):
+        cut = slice(r, r + 256)
+        pair = jnp.zeros((1, 256), F32), jnp.full((1, 256), -jnp.inf, F32)
+        for c in range(0, classes, 1024):
+            size = min(1024, classes - c)
+            scaled = dot(table[c : c + size, :], emb[cut, :], NT) * scale[c // 1024]
+            match = iota((size, 256), 0) == near[:, cut] - c
+            mine = jnp.sum(jnp.where(match, scaled, 0.0), axis=0, keepdims=True)
+            best = jnp.max(jnp.where(match, -1e30, scaled), axis=0, keepdims=True)
+            pair = pair[0] + mine, jnp.maximum(pair[1], best)
+        given.append(pair[0])
+        others.append(pair[1])
+    given, others = jnp.concatenate(given, axis=1), jnp.concatenate(others, axis=1)
     score = (20.0 * (given - others) * inverse_row).astype(BF16).astype(F32)
     lane = (rank + CAP * me[0] + LANES // CORES * away) & (LANES - 1)
     spread = jnp.where(iota((LANES, rows), 0) == lane, score, 0.0).astype(BF16)

time: 62.1 us -> 62.1 us (level)
  no operation moved by 1% of the time
where the time goes in v6:
time: 62.1 us; the launch traced here: 61.9 us
  blocking collectives  47.8 us (77%)
  starting transfers between devices  6.7 us (11%)
  Pallas kernels  6.2 us (10%)
  between operations  0.66 us (1%)
    all_to_all x1, blocking collectives, on_device(): got = lax.all_to_all(sent, CHIPS, 0, 0, tiled=True)  47.8 us
    ppermute x1, starting transfers between devices, on_device(): passed = lax.ppermute(passed, 'core', [(0, 1), (1, 0)])  6.7 us
    pallas_call x1, Pallas kernels, on_device(): pl.pallas_call(functools.partial(pack_kernel, subs), in_specs=[smem, hbm,...  3.74 us
  transfers between devices with their start and end apart: 1, of which 1 were waited for; matrix products, arithmetic and copies ran while one was open for 0% of the time, Pallas kernels for 2%

profile of v6, /device:TPU:513, one launch (start us, length us, event | category | flops | bytes accessed | tf_op | source)
XLA Modules:
  0.0 61.9 jit_solution(15389920507429637346)
XLA Ops:
  0.6 3.7 %pack.1 = bf16[64,2,4736]{2,1,0:T(2,128)(2,1)S(1)} custom-call(s32[1]{0:T(128)} %bitcast.me, s32[1,512]{1,0:T(1,128)} %bitcast.10, s32[1,1000]{1,0:T(1,128)} %bitcast.9, s32[1,512]{1,0:T(1,128)} %bitcast.11, bf16[512,768]{1,0:T(8,128)(2,1)} %emb_hbm.1, bf16[1000,768]{1,0:T(8,128)(2,1)} %table_hbm.1), custom_call_target="tpu_custom_call" | custom-call | tf_op jit(solution)/shard_map/pack/pallas_call | solution.py:224
  4.4 47.8 %all_to_all.5.got = bf16[64,2,4736]{2,1,0:T(2,128)(2,1)S(1)} all-to-all(bf16[64,2,4736]{2,1,0:T(2,128)(2,1)S(1)} %pack.1), channel_id=1, replica_groups=mesh['groups'=2,'x'=8,'core'=2,'sub'=8] {'x','sub'}, dimensions={0} | all-to-all | bytes 2424832 | tf_op jit(solution)/shard_map/all_to_all | solution.py:239
  52.2 0.1 part.1
  52.3 6.7 %collective-permute-start = (bf16[64,2,2432]{2,1,0:T(2,128)(2,1)S(1)}, bf16[64,2,2432]{2,1,0:T(2,128)(2,1)S(1)}, u32[]{:S(2)}, u32[]{:S(2)}) collective-permute-start(bf16[64,2,2432]{2,1,0:T(2,128)(2,1)S(1)} %part.1), channel_id=1, source_target_pairs={{0,8},{8,0},{1,9},{9,1},{2,10},{10,2},{3,11},{11,3},{4,12},{12,4},... | collective-permute-start | bytes 1867784 | tf_op jit(solution)/shard_map/ppermute | solution.py:248
  59.0 1.1 %own.1.own_rows = bf16[8,2,48,768]{3,2,1,0:T(8,128)(2,1)} custom-call(s32[1]{0:T(128)} %bitcast.me, bf16[64,2,4736]{2,1,0:T(2,128)(2,1)S(1)} %all_to_all.5.got), custom_call_target="tpu_custom_call" | custom-call | tf_op jit(solution)/shard_map/own/pallas_call | solution.py:253
  60.1 0.5 collective-permute-done.passed
  60.7 1.2 %passed.1 = (bf16[8,2,48,768]{3,2,1,0:T(8,128)(2,1)}, bf16[6,128]{1,0:T(8,128)(2,1)}, s32[6,128]{1,0:T(8,128)}, s32[1,128]{1,0:T(1,128)}) custom-call(s32[1]{0:T(128)} %bitcast.me, bf16[64,2,4736]{2,1,0:T(2,128)(2,1)S(1)} %all_to_all.5.got, bf16[64,2,2432]{2,1,0:T(2,128)(2,1)S(1)} %collective-permute-done.passed, ...), custom_call_target="tpu_custom_call", output_to_operand_aliasing={{0}: (3, {})} | custom-call | tf_op jit(solution)/shard_map/passed/pallas_call | solution.py:261
Async XLA Ops:
  52.3 8.4 %collective-permute-start = (bf16[64,2,2432]{2,1,0:T(2,128)(2,1)S(1)}, bf16[64,2,2432]{2,1,0:T(2,128)(2,1)S(1)}, u32[]{:S(2)}, u32[]{:S(2)}) collective-permute-start(bf16[64,2,2432]{2,1,0:T(2,128)(2,1)S(1)} %part.1), channel_id=1, source_target_pairs={{0,8},{8,0},{1,9},{9,1},{2,10},{10,2},{3,11},{11,3},{4,12},{12,4},... | collective-permute-start | bytes 1867784 | tf_op jit(solution)/shard_map/ppermute | solution.py:248
